TPU v7x, 32 devices: a whole 2x2x4 slice. The times are simulated.
32 devices in a mesh: rows: 8 (over z, core), aux: 4 (over y, x).
Axes of the slice: x: 2, y: 2, z: 4, core: 2. Of those that a mesh axis runs over, the one named last changes fastest.
Arguments:
- pair_coeffs: float32 [36000, 8192], P('aux', 'rows'), may hold values from -0.0625 to 0.0625
- pair_gaps: float32 [8192], P('rows'), may hold values from 0.2 to 20
- trial_vectors: float32 [36000, 128], P('aux'), may hold values from -0.03125 to 0.03125
Outputs:
- vectors_out: float32 [36000, 128], P('aux')
- rayleigh: float32 [128, 128], replicated
All inputs are finite; a program needn't handle non-finite values.
Results may differ from a plain program's by a relative error of at most 0.00011.
Values sent between devices are 32-bit elements; how exact they have to be, the bound alone decides.
A program may use at most 128 MiB of HBM per device.

v0:
```python
import jax
import jax.numpy as jnp
from jax import lax
from jax.sharding import PartitionSpec as P

ITERS = 2


def project(coeffs, vectors_now):
    return lax.dot_general(
        coeffs,
        vectors_now,
        (((0,), (0,)), ((), ())),
        precision=lax.Precision.HIGHEST,
        preferred_element_type=jnp.float32,
    )


def shards(pair_coeffs, pair_gaps, trial_vectors):
    highest = lax.Precision.HIGHEST
    weights = 4.0 * pair_gaps / (pair_gaps * pair_gaps + 1.0)

    def forward(vectors_now):
        projected = lax.psum(project(pair_coeffs, vectors_now), "aux")
        return (projected, weights)

    vectors_now = trial_vectors
    for step in range(ITERS):
        apply_projected, apply_row_weights = forward(vectors_now)
        scaled = apply_row_weights[:, None] * apply_projected
        partial_sum = jnp.dot(
            pair_coeffs, scaled, precision=highest, preferred_element_type=jnp.float32
        )
        applied = lax.psum(partial_sum, "rows")
        local_gram = jnp.dot(
            applied.T, applied, precision=highest, preferred_element_type=jnp.float32
        )
        correlation = lax.psum(local_gram, "aux")
        factor = jnp.linalg.cholesky(correlation)
        vectors_now = jax.scipy.linalg.solve_triangular(factor, applied.T, lower=True).T
    final_proj, row_weights = forward(vectors_now)
    local_rayleigh = jnp.dot(
        final_proj.T,
        row_weights[:, None] * final_proj,
        precision=highest,
        preferred_element_type=jnp.float32,
    )
    rayleigh = lax.psum(local_rayleigh, "rows")
    return (vectors_now, rayleigh)


def solution(mesh):
    in_specs = (P("aux", "rows"), P("rows"), P("aux", None))
    out_specs = (P("aux", None), P())
    return jax.shard_map(shards, mesh=mesh, in_specs=in_specs, out_specs=out_specs, check_vma=False)
```

profile of v0, /device:TPU:0, one launch (start us, length us, event | category | flops | bytes accessed | tf_op | source)
XLA Modules:
  0.0 741.6 jit_solution(11998312503589431034)
XLA Ops:
  7.2 0.0 copy-start.1
  7.2 0.0 all-reduce.9.cloned.1.call-start
  7.2 27.7 %fusion.19 = f32[1024,128]{0,1:T(8,128)} fusion(f32[9000,1024]{1,0:T(8,128)} %param.6, f32[9000,128]{1,0:T(8,128)} %param.8), kind=kOutput, calls=%fused_computation.33 | convolution fusion | flops 14155776000 | bytes 41996288 | tf_op jit(solution)/shard_map/dot_general | solution.py:10
  34.9 0.0 all-reduce.9.cloned.1.call-update
  34.9 0.0 all-reduce.11.cloned.1.call-start
  35.0 0.0 copy-done.1
  35.0 48.2 %all-reduce.9.cloned.1.call-done = f32[1024,128]{0,1:T(8,128)} async-done(((f32[1024,128]{0,1:T(8,128)}), f32[1024,128]{0,1:T(8,128)}) %all-reduce.9.cloned.1.call-update) | async-done | bytes 524304 | tf_op jit(solution)/shard_map/psum | solution.py:24
  83.2 33.3 %convolution_bitcast_fusion.1 = f32[9000,128]{1,0:T(8,128)} fusion(f32[9000,1024]{1,0:T(8,128)} %param.6, f32[1024,128]{0,1:T(8,128)} %all-reduce.9.cloned.1.call-done, f32[1024]{0:T(1024)S(1)} %add_divide_fusion), kind=kOutput, calls=%fused_computation.1 | convolution fusion | flops 14155907072 | bytes 42000384 | tf_op jit(solution)/shard_map/dot_general | solution.py:31
  116.5 0.0 all-reduce.11.cloned.1.call-update
  116.5 0.3 all-reduce.13.cloned.1.call-start
  116.8 104.8 %all-reduce.11.cloned.1.call-done = f32[9000,128]{1,0:T(8,128)} async-done(((f32[9000,128]{1,0:T(8,128)}), f32[9000,128]{1,0:T(8,128)}) %all-reduce.11.cloned.1.call-update) | async-done | bytes 4608016 | tf_op jit(solution)/shard_map/psum | solution.py:34
  221.5 11.8 %fusion.20 = f32[128,128]{0,1:T(8,128)} fusion(f32[9000,128]{1,0:T(8,128)} %all-reduce.11.cloned.1.call-done), kind=kOutput, calls=%fused_computation.34 | convolution fusion | flops 1769472000 | bytes 4673536 | tf_op jit(solution)/shard_map/dot_general | solution.py:35
  233.3 0.0 all-reduce.13.cloned.1.call-update
  233.3 0.4 all-reduce.15.cloned.1.call-start
  233.8 41.4 %all-reduce.13.cloned.1.call-done = f32[128,128]{0,1:T(8,128)} async-done(((f32[128,128]{0,1:T(8,128)}), f32[128,128]{0,1:T(8,128)}) %all-reduce.13.cloned.1.call-update) | async-done | bytes 65552 | tf_op jit(solution)/shard_map/psum | solution.py:38
  275.1 0.9 copy.6
  276.1 0.9 fusion.16
  276.9 11.7 %cholesky.44 = f32[128,128]{1,0:T(8,128)S(1)} custom-call(f32[128,128]{1,0:T(8,128)S(1)} %fusion.16), custom_call_target="Cholesky" | custom-call | tf_op jit(solution)/shard_map/jit(cholesky)/cholesky | solution.py:39
  288.7 0.6 compare_reduce_fusion.1
  289.3 0.7 fusion.11
  290.0 9.8 %custom-call.6 = f32[1,128,128]{1,2,0:T(8,128)S(1)} custom-call(f32[1,128,128]{2,1,0:T(8,128)S(1)} %fusion.11), custom_call_target="InvertDiagBlocksLowerTriangular" | custom-call | tf_op jit(solution)/shard_map/jit(_solve_triangular)/triangular_solve | solution.py:40
  299.8 6.1 fusion.2
  305.9 24.9 %convolution_bitcast_fusion.2 = f32[1024,128]{0,1:T(8,128)} fusion(f32[128,9000]{1,0:T(8,128)S(1)} %fusion.2, f32[9000,1024]{1,0:T(8,128)} %param.6), kind=kOutput, calls=%fused_computation.6 | convolution fusion | flops 14155776000 | bytes 41996288 | tf_op jit(solution)/shard_map/dot_general | solution.py:10
  330.8 0.0 all-reduce.15.cloned.1.call-update
  330.8 0.2 all-reduce.17.cloned.1.call-start
  331.1 45.3 %all-reduce.15.cloned.1.call-done = f32[1024,128]{0,1:T(8,128)} async-done(((f32[1024,128]{0,1:T(8,128)}), f32[1024,128]{0,1:T(8,128)}) %all-reduce.15.cloned.1.call-update) | async-done | bytes 524304 | tf_op jit(solution)/shard_map/psum | solution.py:24
  376.4 33.3 %convolution_bitcast_fusion = f32[9000,128]{1,0:T(8,128)} fusion(f32[9000,1024]{1,0:T(8,128)} %param.6, f32[1024,128]{0,1:T(8,128)} %all-reduce.15.cloned.1.call-done, f32[1024]{0:T(1024)S(1)} %add_divide_fusion), kind=kOutput, calls=%fused_computation | convolution fusion | flops 14155907072 | bytes 42000384 | tf_op jit(solution)/shard_map/dot_general | solution.py:31
  409.6 0.0 all-reduce.17.cloned.1.call-update
  409.7 0.0 all-reduce.19.cloned.1.call-start
  409.7 105.0 %all-reduce.17.cloned.1.call-done = f32[9000,128]{1,0:T(8,128)} async-done(((f32[9000,128]{1,0:T(8,128)}), f32[9000,128]{1,0:T(8,128)}) %all-reduce.17.cloned.1.call-update) | async-done | bytes 4608016 | tf_op jit(solution)/shard_map/psum | solution.py:34
  514.7 11.8 %fusion.21 = f32[128,128]{0,1:T(8,128)} fusion(f32[9000,128]{1,0:T(8,128)} %all-reduce.17.cloned.1.call-done), kind=kOutput, calls=%fused_computation.35 | convolution fusion | flops 1769472000 | bytes 4673536 | tf_op jit(solution)/shard_map/dot_general | solution.py:35
  526.5 0.0 all-reduce.19.cloned.1.call-update
  526.5 0.3 all-reduce.21.cloned.1.call-start
  526.7 41.5 %all-reduce.19.cloned.1.call-done = f32[128,128]{0,1:T(8,128)} async-done(((f32[128,128]{0,1:T(8,128)}), f32[128,128]{0,1:T(8,128)}) %all-reduce.19.cloned.1.call-update) | async-done | bytes 65552 | tf_op jit(solution)/shard_map/psum | solution.py:38
  568.3 0.9 copy.8
  569.2 0.9 fusion.14
  570.1 11.7 %cholesky.55 = f32[128,128]{1,0:T(8,128)S(1)} custom-call(f32[128,128]{1,0:T(8,128)S(1)} %fusion.14), custom_call_target="Cholesky" | custom-call | tf_op jit(solution)/shard_map/jit(cholesky)/cholesky | solution.py:39
  581.8 0.6 compare_reduce_fusion
  582.5 0.7 fusion.12
  583.1 9.8 %custom-call.7 = f32[1,128,128]{1,2,0:T(8,128)S(1)} custom-call(f32[1,128,128]{2,1,0:T(8,128)S(1)} %fusion.12), custom_call_target="InvertDiagBlocksLowerTriangular" | custom-call | tf_op jit(solution)/shard_map/jit(_solve_triangular)/triangular_solve | solution.py:40
  593.0 9.2 %fusion = f32[128,9000]{0,1:T(8,128)S(1)} fusion(f32[9000,128]{1,0:T(8,128)} %all-reduce.17.cloned.1.call-done, f32[1,128,128]{1,2,0:T(8,128)S(1)} %custom-call.7), kind=kOutput, calls=%fused_computation.2 | convolution fusion | flops 1769472000 | bytes 9281536 | tf_op jit(solution)/shard_map/jit(_solve_triangular)/triangular_solve | solution.py:40
  602.2 0.0 copy-start
  602.2 2.1 copy-done
  604.3 25.4 %convolution_bitcast_fusion.3 = f32[1024,128]{0,1:T(8,128)} fusion(f32[128,9000]{0,1:T(8,128)S(1)} %fusion, f32[9000,1024]{1,0:T(8,128)} %param.6), kind=kOutput, calls=%fused_computation.7 | convolution fusion | flops 14155776000 | bytes 41996288 | tf_op jit(solution)/shard_map/dot_general | solution.py:10
  629.7 0.0 all-reduce.21.cloned.1.call-update
  629.8 0.0 all-reduce.23.cloned.1.call-start
  629.8 45.5 %all-reduce.21.cloned.1.call-done = f32[1024,128]{0,1:T(8,128)} async-done(((f32[1024,128]{0,1:T(8,128)}), f32[1024,128]{0,1:T(8,128)}) %all-reduce.21.cloned.1.call-update) | async-done | bytes 524304 | tf_op jit(solution)/shard_map/psum | solution.py:24
  675.3 2.4 fusion.4
  677.7 0.0 all-reduce.23.cloned.1.call-update
  677.7 55.2 %all-reduce.23.cloned.1.call-done = f32[128,128]{1,0:T(8,128)} async-done(((f32[128,128]{1,0:T(8,128)}), f32[128,128]{1,0:T(8,128)}) %all-reduce.23.cloned.1.call-update) | async-done | bytes 65552 | tf_op jit(solution)/shard_map/psum | solution.py:48
  732.9 1.5 copy.19
  (3 shorter events, 0.1 us)
Async XLA Ops:
  7.2 27.8 %copy-start.1 = (f32[1024]{0:T(1024)S(1)}, f32[1024]{0:T(1024)}, u32[]{:S(2)}) copy-start(f32[1024]{0:T(1024)} %param.7) | copy-start | bytes 12292
  7.2 76.0 %all-reduce.9.cloned.1.call-start = ((), (), s32[]{:S(2)}) async-start(), calls=%async_computation | async-start | bytes 1048576 | tf_op jit(solution)/shard_map/psum | solution.py:24
  34.9 186.6 %all-reduce.11.cloned.1.call-start = ((), (), s32[]{:S(2)}) async-start(), calls=%async_computation.1 | async-start | bytes 9216000 | tf_op jit(solution)/shard_map/psum | solution.py:34
  116.5 158.6 %all-reduce.13.cloned.1.call-start = ((), (), s32[]{:S(2)}) async-start(), calls=%async_computation.2 | async-start | bytes 131072 | tf_op jit(solution)/shard_map/psum | solution.py:38
  233.3 143.0 %all-reduce.15.cloned.1.call-start = ((), (), s32[]{:S(2)}) async-start(), calls=%async_computation.3 | async-start | bytes 1048576 | tf_op jit(solution)/shard_map/psum | solution.py:24
  330.8 183.9 %all-reduce.17.cloned.1.call-start = ((), (), s32[]{:S(2)}) async-start(), calls=%async_computation.4 | async-start | bytes 9216000 | tf_op jit(solution)/shard_map/psum | solution.py:34
  409.7 158.6 %all-reduce.19.cloned.1.call-start = ((), (), s32[]{:S(2)}) async-start(), calls=%async_computation.5 | async-start | bytes 131072 | tf_op jit(solution)/shard_map/psum | solution.py:38
  526.5 148.8 %all-reduce.21.cloned.1.call-start = ((), (), s32[]{:S(2)}) async-start(), calls=%async_computation.6 | async-start | bytes 1048576 | tf_op jit(solution)/shard_map/psum | solution.py:24
  602.2 2.2 copy-start
  629.8 103.1 %all-reduce.23.cloned.1.call-start = ((), (), s32[]{:S(2)}) async-start(), calls=%async_computation.7 | async-start | bytes 131072 | tf_op jit(solution)/shard_map/psum | solution.py:48
Sparse Core Ops, SparseCore 0:
  35.1 48.0 all-reduce.8
  116.6 104.8 all-reduce.10
  233.5 41.6 all-reduce.12
  331.0 45.3 all-reduce.14
  409.8 104.8 all-reduce.16
  526.6 41.6 all-reduce.18
  629.9 45.3 all-reduce.20
  678.2 54.6 all-reduce.22
where the time goes:
time: 748 us; the launch traced here: 742 us
  waiting for transfers between devices  487 us (65%)
  matrix products  186 us (25%)
  other arithmetic  47.4 us (6%)
  between operations  14.6 us (2%)
    psum x2, waiting for transfers between devices, shards(): applied = lax.psum(partial_sum, 'rows')  210 us
    psum x3, waiting for transfers between devices, forward(): projected = lax.psum(project(pair_coeffs, vectors_now), 'aux')  139 us
    psum x2, waiting for transfers between devices, shards(): correlation = lax.psum(local_gram, 'aux')  82.9 us
    dot_general x3, matrix products, project(): lax.dot_general(coeffs, vectors_now, (((0,), (0,)), ((), ())), precision=...  78 us
    dot_general x2, matrix products, shards(): jnp.dot(pair_coeffs, scaled, precision=highest, preferred_element_type=jn...  66.6 us
    psum x1, waiting for transfers between devices, shards(): rayleigh = lax.psum(local_rayleigh, 'rows')  55.2 us
    another operation x6, other arithmetic, shards(): factor = jnp.linalg.cholesky(correlation)  24.8 us
    dot_general x2, matrix products, shards(): jnp.dot(applied.T, applied, precision=highest, preferred_element_type=jnp...  23.5 us
  transfers between devices with their start and end apart: 8, of which 8 were waited for; matrix products, arithmetic and copies ran while one was open for 0% of the time, Pallas kernels for 0%

commit v1 on v0

--- a/solution.py
+++ b/solution.py
@@ -21,7 +21,7 @@
     weights = 4.0 * pair_gaps / (pair_gaps * pair_gaps + 1.0)
 
     def forward(vectors_now):
-        projected = lax.psum(project(pair_coeffs, vectors_now), "aux")
+        projected = jnp.sum(lax.all_gather(project(pair_coeffs, vectors_now), "aux"), axis=0)
         return (projected, weights)
 
     vectors_now = trial_vectors

time: 748 us -> 785 us (1.049)
  matrix products: 186 us -> 239 us
  waiting for transfers between devices: 487 us -> 456 us
    psum x3 -> x0, waiting for transfers between devices: 139 us -> none  [forward(): projected = lax.psum(project(pair_coeffs, vectors_now), 'aux')]
    all_gather x0 -> x3, waiting for transfers between devices: none -> 109 us  [forward(): lax.all_gather(project(pair_coeffs, vectors_now), 'aux')]
    dot_general x3, matrix products: 78 us -> 125 us  [project(): lax.dot_general(coeffs, vectors_now, (((0,), (0,)), ((), ())), precision=...]
where the time goes in v1:
time: 785 us; the launch traced here: 774 us
  waiting for transfers between devices  456 us (58%)
  matrix products  239 us (30%)
  other arithmetic  51.9 us (7%)
  between operations  14.8 us (2%)
  local copies, waits for them, and re-layouts  11.7 us (1%)
    psum x2, waiting for transfers between devices, shards(): applied = lax.psum(partial_sum, 'rows')  210 us
    dot_general x3, matrix products, project(): lax.dot_general(coeffs, vectors_now, (((0,), (0,)), ((), ())), precision=...  125 us
    all_gather x3, waiting for transfers between devices, forward(): lax.all_gather(project(pair_coeffs, vectors_now), 'aux')  109 us
    psum x2, waiting for transfers between devices, shards(): correlation = lax.psum(local_gram, 'aux')  83.1 us
    dot_general x2, matrix products, shards(): jnp.dot(pair_coeffs, scaled, precision=highest, preferred_element_type=jn...  69.5 us
    psum x1, waiting for transfers between devices, shards(): rayleigh = lax.psum(local_rayleigh, 'rows')  54.8 us
    another operation x6, other arithmetic, shards(): factor = jnp.linalg.cholesky(correlation)  24.8 us
    dot_general x2, matrix products, shards(): jnp.dot(applied.T, applied, precision=highest, preferred_element_type=jnp...  23.5 us
  transfers between devices with their start and end apart: 8, of which 8 were waited for; matrix products, arithmetic and copies ran while one was open for 0% of the time, Pallas kernels for 0%

profile of v1, /device:TPU:0, one launch (start us, length us, event | category | flops | bytes accessed | tf_op | source)
XLA Modules:
  0.0 774.5 jit_solution(10525577226178895978)
XLA Ops:
  7.2 0.0 copy-start.1
  7.2 0.0 all-gather.7.cloned.1.call-start
  7.2 73.7 %fusion.19 = f32[1024,128]{1,0:T(8,128)} fusion(f32[9000,1024]{1,0:T(8,128)} %param.6, f32[9000,128]{1,0:T(8,128)} %param.8), kind=kOutput, calls=%fused_computation.33 | convolution fusion | flops 14155776000 | bytes 41996288 | tf_op jit(solution)/shard_map/dot_general | solution.py:10
  80.9 0.0 all-gather.7.cloned.1.call-update
  81.0 0.0 all-reduce.6.cloned.1.call-start
  81.0 0.0 copy-done.1
  81.0 38.0 %all-gather.7.cloned.1.call-done = f32[4096,128]{1,0:T(8,128)} async-done(((f32[1024,128]{1,0:T(8,128)}), f32[4096,128]{1,0:T(8,128)}) %all-gather.7.cloned.1.call-update) | async-done | bytes 2097168 | tf_op jit(solution)/shard_map/all_gather | solution.py:24
  119.0 1.8 reduce_sum.27
  120.8 34.8 %convolution_bitcast_fusion.1 = f32[9000,128]{1,0:T(8,128)} fusion(f32[9000,1024]{1,0:T(8,128)} %param.6, f32[1024,128]{1,0:T(8,128)S(1)} %reduce_sum.27, f32[1024]{0:T(1024)S(1)} %add_divide_fusion), kind=kOutput, calls=%fused_computation.1 | convolution fusion | flops 14155907072 | bytes 42000384 | tf_op jit(solution)/shard_map/dot_general | solution.py:31
  155.5 0.0 all-reduce.6.cloned.1.call-update
  155.6 0.0 all-reduce.8.cloned.1.call-start
  155.6 105.0 %all-reduce.6.cloned.1.call-done = f32[9000,128]{1,0:T(8,128)} async-done(((f32[9000,128]{1,0:T(8,128)}), f32[9000,128]{1,0:T(8,128)}) %all-reduce.6.cloned.1.call-update) | async-done | bytes 4608016 | tf_op jit(solution)/shard_map/psum | solution.py:34
  260.6 11.8 %fusion.20 = f32[128,128]{0,1:T(8,128)} fusion(f32[9000,128]{1,0:T(8,128)} %all-reduce.6.cloned.1.call-done), kind=kOutput, calls=%fused_computation.34 | convolution fusion | flops 1769472000 | bytes 4673536 | tf_op jit(solution)/shard_map/dot_general | solution.py:35
  272.4 0.0 all-reduce.8.cloned.1.call-update
  272.4 0.3 all-gather.9.cloned.1.call-start
  272.7 41.5 %all-reduce.8.cloned.1.call-done = f32[128,128]{0,1:T(8,128)} async-done(((f32[128,128]{0,1:T(8,128)}), f32[128,128]{0,1:T(8,128)}) %all-reduce.8.cloned.1.call-update) | async-done | bytes 65552 | tf_op jit(solution)/shard_map/psum | solution.py:38
  314.2 0.9 copy.14
  315.1 0.9 fusion.16
  316.0 11.7 %cholesky.44 = f32[128,128]{1,0:T(8,128)S(1)} custom-call(f32[128,128]{1,0:T(8,128)S(1)} %fusion.16), custom_call_target="Cholesky" | custom-call | tf_op jit(solution)/shard_map/jit(cholesky)/cholesky | solution.py:39
  327.7 0.6 compare_reduce_fusion.1
  328.4 0.7 fusion.11
  329.1 9.8 %custom-call.6 = f32[1,128,128]{1,2,0:T(8,128)S(1)} custom-call(f32[1,128,128]{2,1,0:T(8,128)S(1)} %fusion.11), custom_call_target="InvertDiagBlocksLowerTriangular" | custom-call | tf_op jit(solution)/shard_map/jit(_solve_triangular)/triangular_solve | solution.py:40
  338.9 9.6 %fusion.2 = f32[128,9000]{0,1:T(8,128)S(1)} fusion(f32[9000,128]{1,0:T(8,128)} %all-reduce.6.cloned.1.call-done, f32[1,128,128]{1,2,0:T(8,128)S(1)} %custom-call.6), kind=kOutput, calls=%fused_computation.4 | convolution fusion | flops 1769472000 | bytes 9281536 | tf_op jit(solution)/shard_map/jit(_solve_triangular)/triangular_solve | solution.py:40
  348.5 25.7 %convolution_bitcast_fusion.3 = f32[1024,128]{0,1:T(8,128)} fusion(f32[128,9000]{0,1:T(8,128)S(1)} %fusion.2, f32[9000,1024]{1,0:T(8,128)} %param.6), kind=kOutput, calls=%fused_computation.7 | convolution fusion | flops 14155776000 | bytes 41996288 | tf_op jit(solution)/shard_map/dot_general | solution.py:10
  374.2 0.0 all-gather.9.cloned.1.call-update
  374.3 0.0 all-reduce.10.cloned.1.call-start
  374.3 35.3 %all-gather.9.cloned.1.call-done = f32[4096,128]{0,1:T(8,128)} async-done(((f32[1024,128]{0,1:T(8,128)}), f32[4096,128]{0,1:T(8,128)}) %all-gather.9.cloned.1.call-update) | async-done | bytes 2097168 | tf_op jit(solution)/shard_map/all_gather | solution.py:24
  409.6 2.8 reshape.14
  412.4 1.3 reduce_sum.28
  413.8 0.2 copy.15
  414.0 34.8 %convolution_bitcast_fusion = f32[9000,128]{1,0:T(8,128)} fusion(f32[9000,1024]{1,0:T(8,128)} %param.6, f32[1024,128]{1,0:T(8,128)S(1)} %copy.15, f32[1024]{0:T(1024)S(1)} %add_divide_fusion), kind=kOutput, calls=%fused_computation | convolution fusion | flops 14155907072 | bytes 42000384 | tf_op jit(solution)/shard_map/dot_general | solution.py:31
  448.7 0.0 all-reduce.10.cloned.1.call-update
  448.7 0.3 all-reduce.12.cloned.1.call-start
  449.0 104.8 %all-reduce.10.cloned.1.call-done = f32[9000,128]{1,0:T(8,128)} async-done(((f32[9000,128]{1,0:T(8,128)}), f32[9000,128]{1,0:T(8,128)}) %all-reduce.10.cloned.1.call-update) | async-done | bytes 4608016 | tf_op jit(solution)/shard_map/psum | solution.py:34
  553.8 11.8 %fusion.21 = f32[128,128]{0,1:T(8,128)} fusion(f32[9000,128]{1,0:T(8,128)} %all-reduce.10.cloned.1.call-done), kind=kOutput, calls=%fused_computation.35 | convolution fusion | flops 1769472000 | bytes 4673536 | tf_op jit(solution)/shard_map/dot_general | solution.py:35
  565.5 0.0 all-reduce.12.cloned.1.call-update
  565.6 0.3 all-gather.11.cloned.1.call-start
  565.9 41.5 %all-reduce.12.cloned.1.call-done = f32[128,128]{0,1:T(8,128)} async-done(((f32[128,128]{0,1:T(8,128)}), f32[128,128]{0,1:T(8,128)}) %all-reduce.12.cloned.1.call-update) | async-done | bytes 65552 | tf_op jit(solution)/shard_map/psum | solution.py:38
  607.4 0.9 copy.17
  608.3 0.9 fusion.14
  609.2 11.7 %cholesky.55 = f32[128,128]{1,0:T(8,128)S(1)} custom-call(f32[128,128]{1,0:T(8,128)S(1)} %fusion.14), custom_call_target="Cholesky" | custom-call | tf_op jit(solution)/shard_map/jit(cholesky)/cholesky | solution.py:39
  620.9 0.6 compare_reduce_fusion
  621.6 0.7 fusion.12
  622.2 9.8 %custom-call.7 = f32[1,128,128]{1,2,0:T(8,128)S(1)} custom-call(f32[1,128,128]{2,1,0:T(8,128)S(1)} %fusion.12), custom_call_target="InvertDiagBlocksLowerTriangular" | custom-call | tf_op jit(solution)/shard_map/jit(_solve_triangular)/triangular_solve | solution.py:40
  632.0 9.5 %fusion = f32[128,9000]{0,1:T(8,128)S(1)} fusion(f32[9000,128]{1,0:T(8,128)} %all-reduce.10.cloned.1.call-done, f32[1,128,128]{1,2,0:T(8,128)S(1)} %custom-call.7), kind=kOutput, calls=%fused_computation.2 | convolution fusion | flops 1769472000 | bytes 9281536 | tf_op jit(solution)/shard_map/jit(_solve_triangular)/triangular_solve | solution.py:40
  641.6 0.0 copy-start
  641.6 2.1 copy-done
  643.7 25.7 %convolution_bitcast_fusion.2 = f32[1024,128]{0,1:T(8,128)} fusion(f32[128,9000]{0,1:T(8,128)S(1)} %fusion, f32[9000,1024]{1,0:T(8,128)} %param.6), kind=kOutput, calls=%fused_computation.6 | convolution fusion | flops 14155776000 | bytes 41996288 | tf_op jit(solution)/shard_map/dot_general | solution.py:10
  669.5 0.0 all-gather.11.cloned.1.call-update
  669.5 0.0 all-reduce.14.cloned.1.call-start
  669.5 35.3 %all-gather.11.cloned.1.call-done = f32[4096,128]{0,1:T(8,128)} async-done(((f32[1024,128]{0,1:T(8,128)}), f32[4096,128]{0,1:T(8,128)}) %all-gather.11.cloned.1.call-update) | async-done | bytes 2097168 | tf_op jit(solution)/shard_map/all_gather | solution.py:24
  704.8 3.0 reshape.15
  707.8 1.3 reduce_sum.29
  709.1 0.2 copy.18
  709.3 1.4 fusion.4
  710.7 0.0 all-reduce.14.cloned.1.call-update
  710.7 54.8 %all-reduce.14.cloned.1.call-done = f32[128,128]{1,0:T(8,128)} async-done(((f32[128,128]{1,0:T(8,128)}), f32[128,128]{1,0:T(8,128)}) %all-reduce.14.cloned.1.call-update) | async-done | bytes 65552 | tf_op jit(solution)/shard_map/psum | solution.py:48
  765.6 1.5 copy.26
  (3 shorter events, 0.1 us)
Async XLA Ops:
  7.2 73.8 %copy-start.1 = (f32[1024]{0:T(1024)S(1)}, f32[1024]{0:T(1024)}, u32[]{:S(2)}) copy-start(f32[1024]{0:T(1024)} %param.7) | copy-start | bytes 12292
  7.2 111.8 %all-gather.7.cloned.1.call-start = ((), (), s32[]{:S(2)}) async-start(), calls=%async_computation.5 | async-start | bytes 2621440 | tf_op jit(solution)/shard_map/all_gather | solution.py:24
  81.0 179.7 %all-reduce.6.cloned.1.call-start = ((), (), s32[]{:S(2)}) async-start(), calls=%async_computation | async-start | bytes 9216000 | tf_op jit(solution)/shard_map/psum | solution.py:34
  155.6 158.6 %all-reduce.8.cloned.1.call-start = ((), (), s32[]{:S(2)}) async-start(), calls=%async_computation.1 | async-start | bytes 131072 | tf_op jit(solution)/shard_map/psum | solution.py:38
  272.4 137.2 %all-gather.9.cloned.1.call-start = ((), (), s32[]{:S(2)}) async-start(), calls=%async_computation.6 | async-start | bytes 2621440 | tf_op jit(solution)/shard_map/all_gather | solution.py:24
  374.3 179.5 %all-reduce.10.cloned.1.call-start = ((), (), s32[]{:S(2)}) async-start(), calls=%async_computation.2 | async-start | bytes 9216000 | tf_op jit(solution)/shard_map/psum | solution.py:34
  448.7 158.6 %all-reduce.12.cloned.1.call-start = ((), (), s32[]{:S(2)}) async-start(), calls=%async_computation.3 | async-start | bytes 131072 | tf_op jit(solution)/shard_map/psum | solution.py:38
  565.6 139.2 %all-gather.11.cloned.1.call-start = ((), (), s32[]{:S(2)}) async-start(), calls=%async_computation.7 | async-start | bytes 2621440 | tf_op jit(solution)/shard_map/all_gather | solution.py:24
  641.6 2.2 copy-start
  669.5 96.1 %all-reduce.14.cloned.1.call-start = ((), (), s32[]{:S(2)}) async-start(), calls=%async_computation.4 | async-start | bytes 131072 | tf_op jit(solution)/shard_map/psum | solution.py:48
Sparse Core Ops, SparseCore 0:
  81.1 37.8 all-gather.6
  155.7 104.8 all-reduce.5
  272.5 41.6 all-reduce.7
  374.4 35.1 all-gather.8
  448.9 104.8 all-reduce.9
  565.7 41.6 all-reduce.11
  669.6 35.1 all-gather.10
  710.9 54.6 all-reduce.13
